TPU v7x, 32 devices: a whole 2x2x4 slice. The times are simulated.
32 devices in a mesh: pod: 2 (over x), dp: 4 (over z), tp: 4 (over y, core).
Axes of the slice: x: 2, y: 2, z: 4, core: 2. Of those that a mesh axis runs over, the one named last changes fastest.
Arguments:
- x_in: bfloat16 [128, 512, 768], P(('pod', 'dp')), parts along dimension 0
- seg_ids: int32 [128, 512], P(('pod', 'dp')), parts along dimension 0
- gain_one: bfloat16 [768], replicated
- gain_two: bfloat16 [768], replicated
- w_qkv: bfloat16 [768, 2304], P(None, 'tp')
- w_out: bfloat16 [12, 64, 768], P('tp')
- w_up: bfloat16 [768, 3072], P(None, 'tp')
- w_down: bfloat16 [3072, 768], P('tp')
- grad_y: bfloat16 [128, 512, 768], P(('pod', 'dp')), parts along dimension 0
Outputs:
- output 1: bfloat16 [128, 512, 768], P(('pod', 'dp')), parts along dimension 0
- output 2: bfloat16 [128, 512, 768], P(('pod', 'dp')), parts along dimension 0
- output 3: bfloat16 [1536], P('pod'), parts along dimension 0
- output 4: bfloat16 [1536], P('pod'), parts along dimension 0
- output 5: bfloat16 [1536, 2304], P('pod', 'tp'), parts along dimension 0
- output 6: bfloat16 [24, 64, 768], P(('pod', 'tp')), parts along dimension 0
- output 7: bfloat16 [1536, 3072], P('pod', 'tp'), parts along dimension 0
- output 8: bfloat16 [6144, 768], P(('pod', 'tp')), parts along dimension 0
There are 2 independent parts. A program takes and returns all parts, laid end to end along the dimension named above; an argument that names none is the same for every part.
All inputs are finite; a program needn't handle non-finite values.
Results may differ from a plain program's by a relative error of at most 0.0189522.
Values are sent between devices in bfloat16 or wider.
A program may use at most 1 GiB of HBM per device.

v0:
```python
import jax
import jax.numpy as jnp
from jax import lax
from jax.sharding import PartitionSpec as P

EPS_NORM = 1e-5
NEG_LARGE = -1e30


def gelu_tanh(values):
    return jax.nn.gelu(values, approximate=True)


def norm_forward(x_rows, gain_vec):
    x_f32 = x_rows.astype(jnp.float32)
    centered = x_f32 - jnp.mean(x_f32, axis=-1, keepdims=True)
    inv_std = lax.rsqrt(jnp.mean(centered * centered, axis=-1, keepdims=True) + EPS_NORM)
    x_hat = centered * inv_std
    return (x_hat * gain_vec.astype(jnp.float32)).astype(jnp.bfloat16), x_hat, inv_std


def norm_backward(grad_out, x_hat, inv_std, gain_vec):
    grad_f32 = grad_out.astype(jnp.float32)
    grad_gain = jnp.sum(grad_f32 * x_hat, axis=0)
    grad_hat = grad_f32 * gain_vec.astype(jnp.float32)
    mean_one = jnp.mean(grad_hat, axis=-1, keepdims=True)
    mean_two = jnp.mean(grad_hat * x_hat, axis=-1, keepdims=True)
    return inv_std * (grad_hat - mean_one - x_hat * mean_two), grad_gain


def matmul_nt(lhs, rhs):
    return lax.dot_general(lhs, rhs, (((1,), (1,)), ((), ())), preferred_element_type=jnp.float32)


def matmul_tn(lhs, rhs):
    return lax.dot_general(lhs, rhs, (((0,), (0,)), ((), ())), preferred_element_type=jnp.float32)


def attention_forward(q_blk, k_blk, v_blk, allowed, score_scale):
    scores = jnp.einsum("bqnd,bknd->bnqk", q_blk, k_blk, preferred_element_type=jnp.float32) * score_scale
    attn_probs = jax.nn.softmax(jnp.where(allowed, scores, NEG_LARGE), axis=-1)
    attn_out = jnp.einsum("bnqk,bknd->bqnd", attn_probs.astype(jnp.bfloat16), v_blk, preferred_element_type=jnp.float32)
    return attn_out.astype(jnp.bfloat16), attn_probs


def attention_backward(grad_out, q_blk, k_blk, v_blk, attn_probs, score_scale):
    grad_v = jnp.einsum("bnqk,bqnd->bknd", attn_probs.astype(jnp.bfloat16), grad_out, preferred_element_type=jnp.float32)
    grad_probs = jnp.einsum("bqnd,bknd->bnqk", grad_out, v_blk, preferred_element_type=jnp.float32)
    grad_scores = attn_probs * (grad_probs - jnp.sum(grad_probs * attn_probs, axis=-1, keepdims=True))
    grad_low = (grad_scores * score_scale).astype(jnp.bfloat16)
    grad_q = jnp.einsum("bnqk,bknd->bqnd", grad_low, k_blk, preferred_element_type=jnp.float32)
    grad_k = jnp.einsum("bnqk,bqnd->bknd", grad_low, q_blk, preferred_element_type=jnp.float32)
    return grad_q, grad_k, grad_v


def solution(mesh):
    batch_spec = P(("pod", "dp"), None, None)
    seg_spec = P(("pod", "dp"), None)

    def local_step(x_in, seg_ids, gain_one, gain_two, w_qkv, w_out, w_up, w_down, grad_y):
        batch_loc, seq_len, hidden = x_in.shape
        heads_loc = w_out.shape[0]
        head_dim = w_out.shape[1]
        score_scale = head_dim ** -0.5
        tokens = batch_loc * seq_len
        positions = jnp.arange(seq_len)
        allowed = (positions[:, None] >= positions[None, :])[None, None] & (seg_ids[:, None, :, None] == seg_ids[:, None, None, :])
        x_rows = x_in.reshape(tokens, hidden)
        normed_a, hat_a, inv_a = norm_forward(x_rows, gain_one)
        qkv_rows = jnp.dot(normed_a, w_qkv, preferred_element_type=jnp.float32).astype(jnp.bfloat16)
        qkv_rows = qkv_rows.reshape(batch_loc, seq_len, heads_loc, 3, head_dim)
        q_blk = qkv_rows[:, :, :, 0]
        k_blk = qkv_rows[:, :, :, 1]
        v_blk = qkv_rows[:, :, :, 2]
        attn_out, attn_probs = attention_forward(q_blk, k_blk, v_blk, allowed, score_scale)
        attn_rows = attn_out.reshape(tokens, heads_loc, head_dim)
        part_one = lax.dot_general(attn_rows, w_out, (((1, 2), (0, 1)), ((), ())), preferred_element_type=jnp.float32)
        sum_one = lax.psum(part_one.astype(jnp.bfloat16), "tp")
        x_one = (x_rows.astype(jnp.float32) + sum_one.astype(jnp.float32)).astype(jnp.bfloat16)
        normed_b, hat_b, inv_b = norm_forward(x_one, gain_two)
        pre_act = jnp.dot(normed_b, w_up, preferred_element_type=jnp.float32)
        act_val, gelu_pull = jax.vjp(gelu_tanh, pre_act)
        hidden_act = act_val.astype(jnp.bfloat16)
        part_two = jnp.dot(hidden_act, w_down, preferred_element_type=jnp.float32)
        sum_two = lax.psum(part_two.astype(jnp.bfloat16), "tp")
        y_rows = (x_one.astype(jnp.float32) + sum_two.astype(jnp.float32)).astype(jnp.bfloat16)

        grad_rows = grad_y.reshape(tokens, hidden)
        grad_down = matmul_tn(hidden_act, grad_rows)
        grad_hidden = matmul_nt(grad_rows, w_down).astype(jnp.bfloat16)
        grad_pre = gelu_pull(grad_hidden.astype(jnp.float32))[0].astype(jnp.bfloat16)
        grad_up = matmul_tn(normed_b, grad_pre)
        part_b = matmul_nt(grad_pre, w_up).astype(jnp.bfloat16)
        grad_norm_b = lax.psum(part_b, "tp")
        back_b, gain_grad_two = norm_backward(grad_norm_b, hat_b, inv_b, gain_two)
        grad_x_one = (grad_rows.astype(jnp.float32) + back_b).astype(jnp.bfloat16)
        grad_out_w = lax.dot_general(attn_rows, grad_x_one, (((0,), (0,)), ((), ())), preferred_element_type=jnp.float32)
        grad_attn = lax.dot_general(grad_x_one, w_out, (((1,), (2,)), ((), ())), preferred_element_type=jnp.float32).astype(jnp.bfloat16)
        grad_q, grad_k, grad_v = attention_backward(grad_attn.reshape(batch_loc, seq_len, heads_loc, head_dim), q_blk, k_blk, v_blk, attn_probs, score_scale)
        grad_qkv = jnp.stack([grad_q, grad_k, grad_v], axis=3).astype(jnp.bfloat16).reshape(tokens, 3 * heads_loc * head_dim)
        grad_wqkv = matmul_tn(normed_a, grad_qkv)
        part_a = matmul_nt(grad_qkv, w_qkv).astype(jnp.bfloat16)
        grad_norm_a = lax.psum(part_a, "tp")
        back_a, gain_grad_one = norm_backward(grad_norm_a, hat_a, inv_a, gain_one)
        grad_x = (grad_x_one.astype(jnp.float32) + back_a).astype(jnp.bfloat16)

        weight_grads = lax.psum(tuple(grad_mat.astype(jnp.bfloat16) for grad_mat in (grad_wqkv, grad_out_w, grad_up, grad_down)), "dp")
        gain_grads = lax.psum((gain_grad_one, gain_grad_two), "dp")
        return (
            y_rows.reshape(x_in.shape),
            grad_x.reshape(x_in.shape),
            gain_grads[0].astype(jnp.bfloat16),
            gain_grads[1].astype(jnp.bfloat16),
            weight_grads[0],
            weight_grads[1],
            weight_grads[2],
            weight_grads[3],
        )

    return jax.shard_map(
        local_step,
        mesh=mesh,
        in_specs=(batch_spec, seg_spec, P(None), P(None), P(None, "tp"), P("tp", None, None), P(None, "tp"), P("tp", None), batch_spec),
        out_specs=(batch_spec, batch_spec, P("pod"), P("pod"), P("pod", "tp"), P(("pod", "tp"), None, None), P("pod", "tp"), P(("pod", "tp"), None)),
        check_vma=False,
    )
```

profile of v0, /device:TPU:0, one launch (start us, length us, event | category | flops | bytes accessed | tf_op | source)
XLA Modules:
  0.0 1507.7 jit_solution(5762563774577065254)
XLA Ops:
  29.9 14.3 convolution_convert_fusion.4
  44.2 13.7 copy.48
  69.0 28.9 %fusion.108 = (f32[16,3,512]{2,1,0:T(4,128)S(1)}, f32[16,3,512,512]{2,3,1,0:T(8,128)}) fusion(pred[16,512,512]{1,2,0:T(8,128)(4,1)} %compare_and_fusion, bf16[16,512,3,1,64]{1,0,4,3,2:T(8,128)(2,1)} %get-tuple-element.25, bf16[16,512,3,1,64]{1,0,4,3,2:T(8,128)(2,1)} %get-tuple-element.24), kind=kOutput, calls=%fused_computation.129 | convolution fusion | flops 1660944896 | bytes 60915712 | tf_op jit(solution)/shard_map/sub | solution.py:41
  98.6 24.7 %convert_bitcast_fusion = bf16[16,3,8,8,512]{4,3,2,1,0:T(8,128)(2,1)S(1)} fusion(bf16[16,512,3,1,64]{1,0,4,3,2:T(8,128)(2,1)} %get-tuple-element.26, f32[16,3,512,512]{2,3,1,0:T(8,128)} %get-tuple-element.32, f32[16,3,512]{2,1,0:T(4,128)S(1)} %get-tuple-element.31), kind=kOutput, calls=%fused_computation.99 | convolution fusion | flops 1637351424 | bytes 56721408 | tf_op jit(solution)/shard_map/bnqk,bknd->bqnd/dot_general | solution.py:42
  132.4 223.3 %all-reduce.8.cloned.1.call-done = bf16[8192,768]{1,0:T(8,128)(2,1)} async-done(((bf16[8192,768]{1,0:T(8,128)(2,1)}), bf16[8192,768]{1,0:T(8,128)(2,1)}) %all-reduce.8.cloned.1.call-update) | async-done | bytes 12582928 | tf_op jit(solution)/shard_map/psum | solution.py:78
  355.6 14.4 convert_reduce_fusion
  378.2 18.9 %fusion.104 = f32[8192,768]{1,0:T(8,128)} fusion(bf16[768,768]{1,0:T(8,128)(2,1)S(1)} %copy-done, bf16[8192,768]{1,0:T(8,128)(2,1)} %get-tuple-element.23, f32[768]{0:T(1024)S(1)} %convert_element_type.153, f32[8192]{0:T(1024)S(1)} %add_rsqrt_fusion, f32[8192]{0:T(1024)S(1)} %broadcast_multiply_fusion.4), kind=kOutput, calls=%fused_computation.127 | convolution fusion | flops 9695133696 | bytes 38996992 | tf_op jit(solution)/shard_map/dot_general | solution.py:81
  397.1 30.2 %fusion.24 = bf16[8192,768]{1,0:T(8,128)(2,1)} fusion(f32[8192,768]{1,0:T(8,128)} %fusion.104, bf16[8192,768]{1,0:T(8,128)(2,1)} %bitcast.126, bf16[768,768]{1,0:T(8,128)(2,1)S(1)} %copy-done.26), kind=kOutput, calls=%fused_computation.37 | convolution fusion | flops 9802088448 | bytes 51511296 | tf_op jit(solution)/shard_map/dot_general | solution.py:32
  427.3 17.3 %convolution_convert_fusion.1 = bf16[8192,768]{1,0:T(8,128)(2,1)} fusion(bf16[8192,768]{1,0:T(8,128)(2,1)} %fusion.24, bf16[768,768]{1,0:T(8,128)(2,1)S(1)} %copy-done), kind=kOutput, calls=%fused_computation.79 | convolution fusion | flops 9669967872 | bytes 26345472 | tf_op jit(solution)/shard_map/dot_general | solution.py:32
  444.6 22.7 %convolution_convert_fusion.3 = bf16[8192,768]{1,0:T(8,128)(2,1)} fusion(bf16[768,768]{1,0:T(8,128)(2,1)S(1)} %copy-done.26, f32[8192,768]{1,0:T(8,128)} %fusion.104), kind=kOutput, calls=%fused_computation.81 | convolution fusion | flops 9726590976 | bytes 38928384 | tf_op jit(solution)/shard_map/dot_general | solution.py:84
  467.3 198.0 %all-reduce.10.cloned.1.call-done = bf16[8192,768]{1,0:T(8,128)(2,1)} async-done(((bf16[8192,768]{1,0:T(8,128)(2,1)}), bf16[8192,768]{1,0:T(8,128)(2,1)}) %all-reduce.10.cloned.1.call-update) | async-done | bytes 12582928 | tf_op jit(solution)/shard_map/psum | solution.py:94
  665.4 16.4 %fusion.28 = (f32[768]{0:T(1024)}, f32[8192]{0:T(1024)S(1)}, f32[8192]{0:T(1024)S(1)}) fusion(bf16[8192,768]{1,0:T(8,128)(2,1)} %get-tuple-element.23, bf16[8192,768]{1,0:T(8,128)(2,1)} %all-reduce.10.cloned.1.call-done, f32[8192]{0:T(1024)S(1)} %add_rsqrt_fusion, f32[8192]{0:T(1024)S(1)} %broadcast_multiply_fusion.4, f32[768]{0:T(1024)S(1)} %convert_element_type.153), kind=kLoop, calls=%fused_computation.41 | loop fusion | flops 62897408 | bytes 25303040 | tf_op jit(solution)/shard_map/reduce_sum | solution.py:24
  705.2 21.4 %fusion.74 = f32[16,3,512,512]{2,3,1,0:T(8,128)} fusion(bf16[16,512,3,1,64]{1,0,4,3,2:T(8,128)(2,1)} %get-tuple-element.26, bf16[3,8,16,8,512]{4,3,2,1,0:T(8,128)(2,1)} %bitcast.136), kind=kOutput, calls=%fused_computation.94 | convolution fusion | flops 1610612736 | bytes 56623104 | tf_op jit(solution)/shard_map/bqnd,bknd->bnqk/dot_general | solution.py:48
  726.6 64.4 %fusion.83 = bf16[16,512,3,1,64]{1,4,2,0,3:T(8,128)(2,1)} fusion(f32[16,3,512,512]{2,3,1,0:T(8,128)} %fusion.74, bf16[16,512,3,1,64]{1,0,4,3,2:T(8,128)(2,1)} %get-tuple-element.24, f32[16,3,512,512]{2,3,1,0:T(8,128)} %get-tuple-element.32, f32[16,3,512]{2,1,0:T(4,128)S(1)} %copy-done.32), kind=kOutput, calls=%fused_computation.103 | convolution fusion | flops 1698718208 | bytes 107053056 | tf_op jit(solution)/shard_map/bnqk,bknd->bqnd/dot_general | solution.py:51
  791.1 63.8 %fusion.86 = bf16[16,512,3,1,64]{1,4,2,0,3:T(8,128)(2,1)} fusion(f32[16,3,512,512]{2,3,1,0:T(8,128)} %fusion.74, bf16[16,512,3,1,64]{1,0,4,3,2:T(8,128)(2,1)} %get-tuple-element.25, f32[16,3,512,512]{2,3,1,0:T(8,128)} %get-tuple-element.32, f32[16,3,512]{2,1,0:T(4,128)S(1)} %copy-done.32), kind=kOutput, calls=%fused_computation.104 | convolution fusion | flops 1698718208 | bytes 107053056 | tf_op jit(solution)/shard_map/bnqk,bqnd->bknd/dot_general | solution.py:52
  854.9 20.8 %fusion.78 = bf16[16,512,3,1,64]{1,4,2,0,3:T(8,128)(2,1)} fusion(bf16[3,8,16,8,512]{4,3,2,1,0:T(8,128)(2,1)} %bitcast.137, f32[16,3,512,512]{2,3,1,0:T(8,128)} %get-tuple-element.32, f32[16,3,512]{2,1,0:T(4,128)S(1)} %copy-done.32), kind=kOutput, calls=%fused_computation.102 | convolution fusion | flops 1635778560 | bytes 56721408 | tf_op jit(solution)/shard_map/bnqk,bqnd->bknd/dot_general | solution.py:47
  897.5 18.4 %copy.49 = bf16[72,8,16,512]{3,1,2,0:T(8,128)(2,1)} copy(bf16[72,8,16,512]{3,2,1,0:T(8,128)(2,1)} %bitcast.125) | data formatting | bytes 18874368
  916.0 16.5 %convolution_convert_fusion = bf16[8192,768]{1,0:T(8,128)(2,1)} fusion(bf16[8192,576]{0,1:T(8,128)(2,1)} %bitcast.133, bf16[768,576]{0,1:T(8,128)(2,1)S(1)} %copy-done.28), kind=kOutput, calls=%fused_computation.78 | convolution fusion | flops 7254048768 | bytes 22904832 | tf_op jit(solution)/shard_map/dot_general | solution.py:32
  945.5 19.9 %convolution_convert_fusion.6 = bf16[768,768]{1,0:T(8,128)(2,1)} fusion(bf16[8192,768]{1,0:T(8,128)(2,1)} %fusion.24, bf16[8192,768]{1,0:T(8,128)(2,1)} %get-tuple-element.23, f32[768]{0:T(1024)S(1)} %copy-done.22, f32[8192]{0:T(1024)S(1)} %copy-done.16, f32[8192]{0:T(1024)S(1)} %copy-done.12), kind=kOutput, calls=%fused_computation.107 | convolution fusion | flops 9695723520 | bytes 26414080 | tf_op jit(solution)/shard_map/dot_general | solution.py:36
  965.4 19.6 %convolution_convert_fusion.5 = bf16[768,768]{1,0:T(8,128)(2,1)} fusion(bf16[8192,768]{1,0:T(8,128)(2,1)} %bitcast.127, f32[8192,768]{1,0:T(8,128)} %fusion.104), kind=kOutput, calls=%fused_computation.106 | convolution fusion | flops 9720889344 | bytes 38928384 | tf_op jit(solution)/shard_map/dot_general | solution.py:36
  1004.0 351.7 %all-reduce.12.cloned.1.call-done = (bf16[8192,768]{1,0:T(8,128)(2,1)}, bf16[8192,768]{1,0:T(8,128)(2,1)}) async-done(((bf16[8192,768]{1,0:T(8,128)(2,1)}, bf16[8192,768]{1,0:T(8,128)(2,1)}), (bf16[8192,768]{1,0:T(8,128)(2,1)}, bf16[8192,768]{1,0:T(8,128)(2,1)})) %all-reduce.12.cloned.1.call-update) | async-done | bytes 25165840 | tf_op jit(solution)/shard_map/psum | solution.py:85
  1355.7 15.1 %fusion.34 = (f32[768]{0:T(1024)S(1)}, f32[8192]{0:T(1024)S(1)}, f32[8192]{0:T(1024)S(1)}) fusion(bf16[8192,768]{1,0:T(8,128)(2,1)} %get-tuple-element.17, bf16[16,512,768]{2,1,0:T(8,128)(2,1)} %param.9, f32[8192]{0:T(1024)S(1)} %bitcast.141, f32[8192]{0:T(1024)S(1)} %bitcast.144, f32[768]{0:T(1024)S(1)} %copy-done.20), kind=kLoop, calls=%fused_computation.47 | loop fusion | flops 62897408 | bytes 25303040 | tf_op jit(solution)/shard_map/reduce_sum | solution.py:24
  1395.3 20.9 %fusion.32 = bf16[8192,768]{1,0:T(8,128)(2,1)} fusion(bf16[8192,768]{1,0:T(8,128)(2,1)} %get-tuple-element.17, bf16[16,512,768]{2,1,0:T(8,128)(2,1)} %param.9, bf16[8192,768]{1,0:T(8,128)(2,1)} %copy-done.3, f32[8192]{0:T(1024)S(1)} %broadcast_multiply_fusion, f32[8192]{0:T(1024)S(1)} %broadcast_multiply_fusion.1, f32[768]{0:T(1024)S(1)} %copy-done.20, ...), kind=kLoop, calls=%fused_computation.45 | loop fusion | flops 75497472 | bytes 50465792 | tf_op jit(solution)/shard_map/convert_element_type | solution.py:105
  1416.2 75.9 %all-reduce.14.cloned.1.call-done = (bf16[768,576]{0,1:T(8,128)(2,1)}, bf16[3,64,768]{2,1,0:T(8,128)(2,1)}, bf16[768,768]{1,0:T(8,128)(2,1)}, bf16[768,768]{1,0:T(8,128)(2,1)}) async-done(((bf16[768,576]{0,1:T(8,128)(2,1)}, bf16[3,64,768]{2,1,0:T(8,128)(2,1)}, bf16[768,768]{1,0:T(8,128)(2,1)}, bf16[768,768]{1,0:T(8,128)(2,1)}), (bf16[768,576]{0,1:T(8,128)(2,1)}, bf16[3,64,768]{2,1,0:T(8,128)(2,1)}, ...) | async-done | bytes 3538960 | tf_op jit(solution)/shard_map/psum | solution.py:107
  (114 shorter events, 161.7 us)
Async XLA Ops:
  7.2 371.0 %copy-start = (bf16[768,768]{1,0:T(8,128)(2,1)S(1)}, bf16[768,768]{1,0:T(8,128)(2,1)}, u32[]{:S(2)}) copy-start(bf16[768,768]{1,0:T(8,128)(2,1)} %param.15) | copy-start | bytes 3538948
  7.2 348.4 %all-reduce.8.cloned.1.call-start = ((), (), s32[]{:S(2)}) async-start(), calls=%async_computation | async-start | bytes 25165824 | tf_op jit(solution)/shard_map/psum | solution.py:78
  7.3 22.5 %copy-start.27 = (bf16[768,576]{0,1:T(8,128)(2,1)S(1)}, bf16[768,576]{0,1:T(8,128)(2,1)}, u32[]{:S(2)}) copy-start(bf16[768,576]{0,1:T(8,128)(2,1)} %param.13) | copy-start | bytes 2654212
  13.8 30.4 %copy-start.13 = (f32[16,512]{1,0:T(8,128)}, f32[16,512]{1,0:T(8,128)S(1)}, u32[]{:S(2)}) copy-start(f32[16,512]{1,0:T(8,128)S(1)} %get-tuple-element.30) | copy-start | bytes 98308
  22.6 21.5 %copy-start.7 = (f32[2,4,8,128]{3,1,2,0:T(4,128)}, f32[2,4,8,128]{3,1,2,0:T(4,128)S(1)}, u32[]{:S(2)}) copy-start(f32[2,4,8,128]{3,1,2,0:T(4,128)S(1)} %copy.47) | copy-start | bytes 98308
  22.7 21.5 %copy-start.9 = (f32[2,4,8,128]{3,1,2,0:T(4,128)}, f32[2,4,8,128]{3,1,2,0:T(4,128)S(1)}, u32[]{:S(2)}) copy-start(f32[2,4,8,128]{3,1,2,0:T(4,128)S(1)} %copy.46) | copy-start | bytes 98308
  22.7 21.5 %copy-start.19 = (f32[768]{0:T(1024)}, f32[768]{0:T(1024)S(1)}, u32[]{:S(2)}) copy-start(f32[768]{0:T(1024)S(1)} %convert_element_type.143) | copy-start | bytes 9220
  44.2 20.2 %copy-start.17 = (s32[16,512]{1,0:T(8,128)S(1)}, s32[16,512]{1,0:T(8,128)}, u32[]{:S(2)}) copy-start(s32[16,512]{1,0:T(8,128)} %param.10) | copy-start | bytes 98308
  98.6 26.8 %copy-start.29 = (bf16[3,64,768]{2,1,0:T(8,128)(2,1)S(1)}, bf16[3,64,768]{2,1,0:T(8,128)(2,1)}, u32[]{:S(2)}) copy-start(bf16[3,64,768]{2,1,0:T(8,128)(2,1)} %param.14) | copy-start | bytes 884740
  132.3 533.1 %all-reduce.10.cloned.1.call-start = ((), (), s32[]{:S(2)}) async-start(), calls=%async_computation.1 | async-start | bytes 25165824 | tf_op jit(solution)/shard_map/psum | solution.py:94
  132.4 549.4 %copy-start.21 = (f32[768]{0:T(1024)}, f32[768]{0:T(1024)S(1)}, u32[]{:S(2)}) copy-start(f32[768]{0:T(1024)S(1)} %convert_element_type.153) | copy-start | bytes 9220
  370.0 311.8 %copy-start.11 = (f32[8192]{0:T(1024)}, f32[8192]{0:T(1024)S(1)}, u32[]{:S(2)}) copy-start(f32[8192]{0:T(1024)S(1)} %broadcast_multiply_fusion.4) | copy-start | bytes 98308
  378.2 303.6 %copy-start.15 = (f32[8192]{0:T(1024)}, f32[8192]{0:T(1024)S(1)}, u32[]{:S(2)}) copy-start(f32[8192]{0:T(1024)S(1)} %add_rsqrt_fusion) | copy-start | bytes 98308
  378.2 18.9 %copy-start.26 = (bf16[768,768]{1,0:T(8,128)(2,1)S(1)}, bf16[768,768]{1,0:T(8,128)(2,1)}, u32[]{:S(2)}) copy-start(bf16[768,768]{1,0:T(8,128)(2,1)} %param.16) | copy-start | bytes 3538948
  444.6 911.1 %all-reduce.12.cloned.1.call-start = ((), (), s32[]{:S(2)}) async-start(), calls=%async_computation.2 | async-start | bytes 50331648 | tf_op jit(solution)/shard_map/psum | solution.py:85
  681.8 17.9 %copy-start.30 = (bf16[3,64,768]{2,1,0:T(8,128)(2,1)S(1)}, bf16[3,64,768]{2,1,0:T(8,128)(2,1)}, u32[]{:S(2)}) copy-start(bf16[3,64,768]{2,1,0:T(8,128)(2,1)} %param.14) | copy-start | bytes 884740
  705.2 21.5 %copy-start.32 = (f32[16,3,512]{2,1,0:T(4,128)S(1)}, f32[16,3,512]{2,1,0:T(4,128)}, u32[]{:S(2)}) copy-start(f32[16,3,512]{2,1,0:T(4,128)} %copy-done.31) | copy-start | bytes 294916
  875.7 40.3 %copy-start.28 = (bf16[768,576]{0,1:T(8,128)(2,1)S(1)}, bf16[768,576]{0,1:T(8,128)(2,1)}, u32[]{:S(2)}) copy-start(bf16[768,576]{0,1:T(8,128)(2,1)} %param.13) | copy-start | bytes 2654212
  932.6 559.6 %all-reduce.14.cloned.1.call-start = ((), (), s32[]{:S(2)}) async-start(), calls=%async_computation.3 | async-start | bytes 7077888 | tf_op jit(solution)/shard_map/psum | solution.py:107
  965.4 19.6 %copy-start.6 = (bf16[16,3,8,8,512]{4,3,0,2,1:T(8,128)(2,1)S(1)}, bf16[16,3,8,8,512]{4,3,0,2,1:T(8,128)(2,1)}, u32[]{:S(2)}) copy-start(bf16[16,3,8,8,512]{4,3,0,2,1:T(8,128)(2,1)} %copy-done.5) | copy-start | bytes 9437188
  965.4 27.6 %copy-start.4 = (bf16[16,512,768]{2,1,0:T(8,128)(2,1)S(1)}, bf16[16,512,768]{2,1,0:T(8,128)(2,1)}, u32[]{:S(2)}) copy-start(bf16[16,512,768]{2,1,0:T(8,128)(2,1)} %fusion.45) | copy-start | bytes 37748740
  993.0 362.6 %copy-start.8 = (f32[2,4,8,128]{3,1,2,0:T(4,128)S(1)}, f32[2,4,8,128]{3,1,2,0:T(4,128)}, u32[]{:S(2)}) copy-start(f32[2,4,8,128]{3,1,2,0:T(4,128)} %copy-done.7) | copy-start | bytes 98308
  993.0 362.6 %copy-start.10 = (f32[2,4,8,128]{3,1,2,0:T(4,128)S(1)}, f32[2,4,8,128]{3,1,2,0:T(4,128)}, u32[]{:S(2)}) copy-start(f32[2,4,8,128]{3,1,2,0:T(4,128)} %copy-done.9) | copy-start | bytes 98308
  1395.3 105.4 %copy-start.1 = (bf16[768,768]{1,0:T(8,128)(2,1)S(1)}, bf16[768,768]{1,0:T(8,128)(2,1)}, u32[]{:S(2)}) copy-start(bf16[768,768]{1,0:T(8,128)(2,1)} %param.15) | copy-start | bytes 3538948
  (16 other events, 146.1 us)
Sparse Core Ops, SparseCore 0:
  132.4 223.1 all-reduce.7
  444.7 220.6 all-reduce.9
  932.7 422.9 all-reduce.11
  1358.7 133.4 all-reduce.13
where the time goes:
time: 1510 us
  waiting for transfers between devices  849 us (56%)
  matrix products  415 us (27%)
  other arithmetic  148 us (10%)
  local copies, waits for them, and re-layouts  68.6 us (5%)
    psum x1, waiting for transfers between devices, local_step(): sum_two = lax.psum(part_two.astype(jnp.bfloat16), 'tp')  352 us
    psum x1, waiting for transfers between devices, local_step(): sum_one = lax.psum(part_one.astype(jnp.bfloat16), 'tp')  223 us
    psum x1, waiting for transfers between devices, local_step(): grad_norm_b = lax.psum(part_b, 'tp')  198 us
    psum x1, waiting for transfers between devices, local_step(): lax.psum(tuple((grad_mat.astype(jnp.bfloat16) for grad_mat in (grad_wqkv,...  75.9 us
    dot_general x1, matrix products, attention_backward(): jnp.einsum('bnqk,bknd->bqnd', grad_low, k_blk, preferred_element_type=jnp...  64.4 us
    dot_general x3, matrix products, matmul_nt(): lax.dot_general(lhs, rhs, (((1,), (1,)), ((), ())), preferred_element_typ...  64 us
    dot_general x1, matrix products, attention_backward(): jnp.einsum('bnqk,bqnd->bknd', grad_low, q_blk, preferred_element_type=jnp...  63.8 us
    dot_general x3, matrix products, matmul_tn(): lax.dot_general(lhs, rhs, (((0,), (0,)), ((), ())), preferred_element_typ...  50.5 us
  transfers between devices with their start and end apart: 4, of which 4 were waited for; matrix products, arithmetic and copies ran while one was open for 9% of the time, Pallas kernels for 0%

commit v1 on v0

v1 whole, which is shorter than its diff:
```python
import functools

import jax
import jax.numpy as jnp
from jax import lax
from jax.experimental import pallas as pl
from jax.experimental.pallas import tpu as pltpu
from jax.sharding import PartitionSpec as P


EPS_NORM = 1e-5
MASKED = -1e30
OPEN = 3e38
LOG2E = 1.4426950408889634
NT = (((1,), (1,)), ((), ()))
TN = (((0,), (0,)), ((), ()))
NN = (((1,), (0,)), ((), ()))
HEADS_PER_STEP = 2
PLACE_ROWS = 512
GAIN_ROWS = 64


def dot32(lhs, rhs, dims):
    return lax.dot_general(lhs, rhs, dims, preferred_element_type=jnp.float32)


def norm_forward(x_rows, gain_vec):
    x_f32 = x_rows.astype(jnp.float32)
    centered = x_f32 - jnp.mean(x_f32, axis=-1, keepdims=True)
    inv_std = lax.rsqrt(jnp.mean(centered * centered, axis=-1, keepdims=True) + EPS_NORM)
    x_hat = centered * inv_std
    return (x_hat * gain_vec.astype(jnp.float32)).astype(jnp.bfloat16), x_hat, inv_std


def norm_backward(grad_out, x_hat, inv_std, gain_vec):
    grad_f32 = grad_out.astype(jnp.float32)
    grad_gain = jnp.sum(grad_f32 * x_hat, axis=0)
    grad_hat = grad_f32 * gain_vec.astype(jnp.float32)
    mean_one = jnp.mean(grad_hat, axis=-1, keepdims=True)
    mean_two = jnp.mean(grad_hat * x_hat, axis=-1, keepdims=True)
    return inv_std * (grad_hat - mean_one - x_hat * mean_two), grad_gain


def fill_limit(seg_q_ref, seg_k_ref, limit_ref):
    seq = limit_ref.shape[0]
    key_pos = lax.broadcasted_iota(jnp.int32, (seq, seq), 0)
    query_pos = lax.broadcasted_iota(jnp.int32, (seq, seq), 1)
    allowed = (key_pos <= query_pos) & (seg_k_ref[0] == seg_q_ref[0])
    limit_ref[...] = jnp.where(allowed, OPEN, MASKED)


def attn_fwd_kernel(head_dim, score_scale, seg_q_ref, seg_k_ref, qkv_ref, out_ref, lse_ref, limit_ref):
    @pl.when(pl.program_id(1) == 0)
    def _():
        fill_limit(seg_q_ref, seg_k_ref, limit_ref)

    seq = limit_ref.shape[0]
    half = seq // 2
    factor = score_scale * LOG2E
    for head in range(HEADS_PER_STEP):
        base = head * 3 * head_dim
        q_t = qkv_ref[base : base + head_dim, :]
        k_t = qkv_ref[base + head_dim : base + 2 * head_dim, :]
        v_t = qkv_ref[base + 2 * head_dim : base + 3 * head_dim, :]
        for blk in range(2):
            keys = (blk + 1) * half
            cols = slice(blk * half, (blk + 1) * half)
            raw = dot32(k_t[:, :keys], q_t[:, cols], TN)
            raw = jnp.minimum(raw, limit_ref[:keys, cols])
            top = jnp.max(raw, axis=0, keepdims=True)
            weights = jnp.exp2((raw - top) * factor)
            total = jnp.sum(weights, axis=0, keepdims=True)
            out = dot32(v_t[:, :keys], weights.astype(jnp.bfloat16), NN)
            out_ref[head * head_dim : (head + 1) * head_dim, cols] = (out / total).astype(jnp.bfloat16)
            lse_ref[0, 0, head : head + 1, cols] = top * factor + jnp.log2(total)


def attn_bwd_kernel(head_dim, score_scale, seg_q_ref, seg_k_ref, qkv_ref, out_ref, lse_ref, grad_ref, dqkv_ref, limit_ref):
    @pl.when(pl.program_id(1) == 0)
    def _():
        fill_limit(seg_q_ref, seg_k_ref, limit_ref)

    seq = limit_ref.shape[0]
    half = seq // 2
    factor = score_scale * LOG2E
    for head in range(HEADS_PER_STEP):
        base = head * 3 * head_dim
        q_t = qkv_ref[base : base + head_dim, :]
        k_t = qkv_ref[base + head_dim : base + 2 * head_dim, :]
        v_t = qkv_ref[base + 2 * head_dim : base + 3 * head_dim, :]
        g_t = grad_ref[head * head_dim : (head + 1) * head_dim, :]
        o_t = out_ref[head * head_dim : (head + 1) * head_dim, :]
        delta = jnp.sum(g_t.astype(jnp.float32) * o_t.astype(jnp.float32), axis=0, keepdims=True)
        grads_k, grads_v = [], []
        for blk in range(2):
            keys = (blk + 1) * half
            cols = slice(blk * half, (blk + 1) * half)
            raw = dot32(k_t[:, :keys], q_t[:, cols], TN)
            raw = jnp.minimum(raw, limit_ref[:keys, cols])
            probs = jnp.exp2(raw * factor - lse_ref[0, 0, head : head + 1, cols])
            grad_p = dot32(v_t[:, :keys], g_t[:, cols], TN)
            grad_s = (probs * (grad_p - delta[:, cols])).astype(jnp.bfloat16)
            grads_v.append(dot32(g_t[:, cols], probs.astype(jnp.bfloat16), NT))
            grads_k.append(dot32(q_t[:, cols], grad_s, NT))
            grad_q = dot32(k_t[:, :keys], grad_s, NN) * score_scale
            dqkv_ref[base : base + head_dim, cols] = grad_q.astype(jnp.bfloat16)
        for pos, (low, full) in enumerate((grads_k, grads_v)):
            scale = score_scale if pos == 0 else 1.0
            start = base + (pos + 1) * head_dim
            dqkv_ref[start : start + head_dim, :half] = ((low + full[:, :half]) * scale).astype(jnp.bfloat16)
            dqkv_ref[start : start + head_dim, half:] = (full[:, half:] * scale).astype(jnp.bfloat16)


def attn_specs(head_dim, seq):
    step_rows = HEADS_PER_STEP * head_dim
    return {
        "seg_q": pl.BlockSpec((1, 1, seq), lambda b, h: (b, 0, 0)),
        "seg_k": pl.BlockSpec((1, seq, 1), lambda b, h: (b, 0, 0)),
        "qkv": pl.BlockSpec((3 * step_rows, seq), lambda b, h: (h, b)),
        "out": pl.BlockSpec((step_rows, seq), lambda b, h: (h, b)),
        "lse": pl.BlockSpec((1, 1, HEADS_PER_STEP, seq), lambda b, h: (b, h, 0, 0)),
    }


def attention_forward(seg_q, seg_k, qkv_t, batch, heads, head_dim, seq):
    specs = attn_specs(head_dim, seq)
    groups = heads // HEADS_PER_STEP
    return pl.pallas_call(
        functools.partial(attn_fwd_kernel, head_dim, head_dim ** -0.5),
        grid=(batch, groups),
        in_specs=[specs["seg_q"], specs["seg_k"], specs["qkv"]],
        out_specs=[specs["out"], specs["lse"]],
        out_shape=[
            jax.ShapeDtypeStruct((heads * head_dim, batch * seq), jnp.bfloat16),
            jax.ShapeDtypeStruct((batch, groups, HEADS_PER_STEP, seq), jnp.float32),
        ],
        scratch_shapes=[pltpu.VMEM((seq, seq), jnp.float32)],
        cost_estimate=pl.CostEstimate(flops=batch * heads * seq * seq * head_dim * 16, bytes_accessed=12 << 20, transcendentals=batch * heads * seq * seq),
        name="attn_fwd",
    )(seg_q, seg_k, qkv_t)


def attention_backward(seg_q, seg_k, qkv_t, out_t, lse, grad_t, batch, heads, head_dim, seq):
    specs = attn_specs(head_dim, seq)
    return pl.pallas_call(
        functools.partial(attn_bwd_kernel, head_dim, head_dim ** -0.5),
        grid=(batch, heads // HEADS_PER_STEP),
        in_specs=[specs["seg_q"], specs["seg_k"], specs["qkv"], specs["out"], specs["lse"], specs["out"]],
        out_specs=specs["qkv"],
        out_shape=jax.ShapeDtypeStruct((3 * heads * head_dim, batch * seq), jnp.bfloat16),
        scratch_shapes=[pltpu.VMEM((seq, seq), jnp.float32)],
        cost_estimate=pl.CostEstimate(flops=batch * heads * seq * seq * head_dim * 40, bytes_accessed=24 << 20, transcendentals=batch * heads * seq * seq),
        name="attn_bwd",
    )(seg_q, seg_k, qkv_t, out_t, lse, grad_t)


def place_kernel(slots_ref, one_ref, two_ref, *rest):
    out_ref = rest[-1]

    @pl.when(pl.program_id(0) == 0)
    def _():
        out_ref[0] = one_ref[...]

    @pl.when(pl.program_id(0) == 1)
    def _():
        out_ref[0] = two_ref[...]


def place_pair(slots, one, two, slot_count, base=None):
    rows, width = one.shape
    chunks = rows // PLACE_ROWS
    last = chunks - 1
    block = (PLACE_ROWS, width)
    in_specs = [
        pl.BlockSpec(block, lambda s, c, slots: (jnp.where(s == 0, c, last), 0)),
        pl.BlockSpec(block, lambda s, c, slots: (jnp.where(s == 0, 0, c), 0)),
    ]
    operands = [slots, one, two]
    aliases = {}
    if base is not None:
        in_specs.append(pl.BlockSpec(memory_space=pl.ANY))
        operands.append(base)
        aliases = {3: 0}
    return pl.pallas_call(
        place_kernel,
        grid_spec=pltpu.PrefetchScalarGridSpec(
            num_scalar_prefetch=1,
            grid=(2, chunks),
            in_specs=in_specs,
            out_specs=pl.BlockSpec((1,) + block, lambda s, c, slots: (slots[s], c, 0)),
        ),
        out_shape=jax.ShapeDtypeStruct((slot_count, rows, width), one.dtype),
        input_output_aliases=aliases,
        cost_estimate=pl.CostEstimate(flops=0, bytes_accessed=4 * rows * width * 2, transcendentals=0),
        name="place_pair",
    )(*operands)


def add_low(*parts):
    total = parts[0].astype(jnp.float32)
    for part in parts[1:]:
        total = total + part.astype(jnp.float32)
    return total.astype(jnp.bfloat16)


def ring_sum(mat, axis, size):
    rows = mat.shape[0] // size
    half = rows // 32 * 16
    me = lax.axis_index(axis)
    upward = [(i, (i + 1) % size) for i in range(size)]
    downward = [(i, (i - 1) % size) for i in range(size)]
    chunks = mat.reshape(size, rows, mat.shape[1])
    own, following, opposite, previous = (
        lax.dynamic_index_in_dim(chunks, lax.rem(me + k, size), 0, keepdims=False) for k in range(size)
    )
    low = lax.ppermute(opposite[:half], axis, upward)
    high = lax.ppermute(opposite[half:], axis, downward)
    to_next = jnp.concatenate([add_low(following[:half], low), following[half:]])
    to_previous = jnp.concatenate([previous[:half], add_low(previous[half:], high)])
    from_previous = lax.ppermute(to_next, axis, upward)
    from_next = lax.ppermute(to_previous, axis, downward)
    total = add_low(own, from_previous, from_next)
    have_previous = lax.ppermute(total, axis, upward)
    have_next = lax.ppermute(total, axis, downward)
    far_low = lax.ppermute(have_previous[:half], axis, upward)
    far_high = lax.ppermute(have_next[half:], axis, downward)
    whole = jnp.zeros_like(mat)
    far_row = lax.rem(me + 2, size) * rows
    for block, row in (
        (total, me * rows),
        (have_next, lax.rem(me + 1, size) * rows),
        (have_previous, lax.rem(me + size - 1, size) * rows),
        (far_low, far_row),
        (far_high, far_row + half),
    ):
        whole = lax.dynamic_update_slice_in_dim(whole, block, row, 0)
    return whole


def gelu_tanh(values):
    return jax.nn.gelu(values, approximate=True)


def solution(mesh):
    tp_size = mesh.shape["tp"]
    dp_size = mesh.shape["dp"]
    batch_spec = P(("pod", "dp"), None, None)
    seg_spec = P(("pod", "dp"), None)
    far_pairs = [(i, i ^ 2) for i in range(tp_size)]
    near_pairs = [(i, i ^ 1) for i in range(tp_size)]
    hold = lax.optimization_barrier

    def local_step(x_in, seg_ids, gain_one, gain_two, w_qkv, w_out, w_up, w_down, grad_y):
        batch_loc, seq, hidden = x_in.shape
        heads = w_out.shape[0] * tp_size
        head_dim = w_out.shape[1]
        batch = batch_loc // tp_size
        tokens = batch * seq
        me = lax.axis_index("tp")
        first = me * batch

        def gather(mat):
            return lax.all_gather(mat, "tp", axis=0, tiled=True)

        def scatter(mat):
            return lax.psum_scatter(mat, "tp", scatter_dimension=0, tiled=True)

        def exchange(rows):
            far = lax.ppermute(rows, "tp", far_pairs)
            near = lax.ppermute(rows, "tp", near_pairs)
            far_near = lax.ppermute(far, "tp", near_pairs)
            return near, far, far_near

        def assemble(rows, parts):
            near, far, far_near = parts
            half = place_pair(jnp.stack([me, me ^ 1]), rows, near, tp_size)
            whole = place_pair(jnp.stack([me ^ 2, me ^ 3]), far, far_near, tp_size, half)
            return whole.reshape(x_in.shape)

        wqkv_t = gather(w_qkv.T)
        wout = gather(w_out.reshape(-1, hidden))
        wup_t = gather(w_up.T)
        wdown = gather(w_down)

        x_rows = lax.dynamic_slice_in_dim(x_in, first, batch, 0).reshape(tokens, hidden)
        grad_rows = lax.dynamic_slice_in_dim(grad_y, first, batch, 0).reshape(tokens, hidden)
        seg = lax.dynamic_slice_in_dim(seg_ids, first, batch, 0)
        seg_q, seg_k = seg[:, None, :], seg[:, :, None]

        normed_a, hat_a, inv_a = norm_forward(x_rows, gain_one)
        qkv_t = dot32(wqkv_t, normed_a, NT).astype(jnp.bfloat16)
        out_t, lse = attention_forward(seg_q, seg_k, qkv_t, batch, heads, head_dim, seq)
        part_one = dot32(out_t, wout, TN).astype(jnp.bfloat16)
        x_one = (x_rows.astype(jnp.float32) + part_one.astype(jnp.float32)).astype(jnp.bfloat16)
        normed_b, hat_b, inv_b = norm_forward(x_one, gain_two)
        normed_b = hold(normed_b)
        pre_act = dot32(normed_b, wup_t, NT)
        act_val, gelu_pull = jax.vjp(gelu_tanh, pre_act)
        hidden_act = hold(act_val.astype(jnp.bfloat16))
        part_two = dot32(hidden_act, wdown, NN).astype(jnp.bfloat16)
        y_rows = (x_one.astype(jnp.float32) + part_two.astype(jnp.float32)).astype(jnp.bfloat16)
        y_rows, hidden_act, grad_rows = hold((y_rows, hidden_act, grad_rows))
        y_parts = exchange(y_rows)

        grad_down = dot32(hidden_act, grad_rows, TN).astype(jnp.bfloat16)
        grad_down, grad_rows = hold((grad_down, grad_rows))
        red_down = scatter(grad_down)
        grad_hidden = dot32(grad_rows, wdown, NT).astype(jnp.bfloat16)
        grad_pre = gelu_pull(grad_hidden.astype(jnp.float32))[0].astype(jnp.bfloat16)
        grad_up_t = dot32(grad_pre, normed_b, TN).astype(jnp.bfloat16)
        grad_up_t, grad_pre = hold((grad_up_t, grad_pre))
        red_up_t = scatter(grad_up_t)
        grad_norm_b = dot32(grad_pre, wup_t, NN).astype(jnp.bfloat16)
        back_b, gain_grad_two = norm_backward(grad_norm_b, hat_b, inv_b, gain_two)
        grad_x_one = (grad_rows.astype(jnp.float32) + back_b).astype(jnp.bfloat16)
        grad_out_w = dot32(out_t, grad_x_one, NN).astype(jnp.bfloat16)
        grad_out_w, grad_x_one = hold((grad_out_w, grad_x_one))
        red_out = scatter(grad_out_w)
        grad_attn_t = dot32(wout, grad_x_one, NT).astype(jnp.bfloat16)
        grad_qkv_t = attention_backward(seg_q, seg_k, qkv_t, out_t, lse, grad_attn_t, batch, heads, head_dim, seq)
        grad_norm_a = dot32(grad_qkv_t, wqkv_t, TN).astype(jnp.bfloat16)
        back_a, gain_grad_one = norm_backward(grad_norm_a, hat_a, inv_a, gain_one)
        grad_x = (grad_x_one.astype(jnp.float32) + back_a).astype(jnp.bfloat16)
        grad_x, grad_qkv_t = hold((grad_x, grad_qkv_t))
        grad_x_parts = exchange(grad_x)

        grad_wqkv_t = dot32(grad_qkv_t, normed_a, NN).astype(jnp.bfloat16)
        gains = jnp.stack([gain_grad_one, gain_grad_two]).astype(jnp.bfloat16)
        gains = jnp.pad(gains, ((0, GAIN_ROWS - 2), (0, 0)))
        packed = jnp.concatenate(
            [grad_wqkv_t.reshape(tp_size, -1, hidden), jnp.broadcast_to(gains, (tp_size,) + gains.shape)], axis=1
        ).reshape(-1, hidden)
        packed, red_down, red_up_t, red_out = hold((packed, red_down, red_up_t, red_out))
        red_packed = scatter(packed)
        sum_first = ring_sum(jnp.concatenate([red_down, red_up_t, red_out]), "dp", dp_size)
        sum_packed = ring_sum(red_packed, "dp", dp_size)
        up_start = red_down.shape[0]
        out_start = up_start + red_up_t.shape[0]
        sum_down, sum_up_t, sum_out = sum_first[:up_start], sum_first[up_start:out_start], sum_first[out_start:]
        qkv_rows = w_qkv.shape[1]

        y_full = assemble(y_rows, y_parts)
        grad_x_full = assemble(grad_x, grad_x_parts)
        return (
            y_full,
            grad_x_full,
            sum_packed[qkv_rows],
            sum_packed[qkv_rows + 1],
            sum_packed[:qkv_rows].T,
            sum_out.reshape(w_out.shape),
            sum_up_t.T,
            sum_down,
        )

    return jax.shard_map(
        local_step,
        mesh=mesh,
        in_specs=(batch_spec, seg_spec, P(None), P(None), P(None, "tp"), P("tp", None, None), P(None, "tp"), P("tp", None), batch_spec),
        out_specs=(batch_spec, batch_spec, P("pod"), P("pod"), P("pod", "tp"), P(("pod", "tp"), None, None), P("pod", "tp"), P(("pod", "tp"), None)),
        check_vma=False,
    )
```

time: 1510 us -> 704 us (0.47)
  waiting for transfers between devices: 849 us -> 305 us
  matrix products: 415 us -> 163 us
  other arithmetic: 148 us -> 32.9 us
  Pallas kernels: 0 us -> 112 us
  local copies, waits for them, and re-layouts: 68.6 us -> 37.9 us
  starting transfers between devices: 0.16 us -> 28.8 us
    psum x4 -> x0, waiting for transfers between devices: 849 us -> none  [the longest x1 352 us: local_step(): sum_two = lax.psum(part_two.astype(jnp.bfloat16), 'tp')]
    dot_general x17 -> x12, matrix products: 386 us -> 163 us  [dot32(): return lax.dot_general(lhs, rhs, dims, preferred_element_type=jnp.float32)]
    ppermute x0 -> x22, waiting for transfers between devices: none -> 222 us  [the longest x2 156 us: exchange(): far = lax.ppermute(rows, 'tp', far_pairs)]
    pallas_call x0 -> x6, Pallas kernels: none -> 112 us  [the longest x1 38.7 us: attention_backward(): pl.pallas_call(functools.partial(attn_bwd_kernel, head_dim, head_dim ** (...]
    reduce_scatter x0 -> x4, waiting for transfers between devices: none -> 49.5 us  [scatter(): return lax.psum_scatter(mat, 'tp', scatter_dimension=0, tiled=True)]
    unnamed x80 -> x53, local copies, waits for them, and re-layouts: 48.3 us -> 9.94 us
    reduce_sum x2 -> x0, other arithmetic: 31.5 us -> none  [norm_backward(): grad_gain = jnp.sum(grad_f32 * x_hat, axis=0)]
    all_gather x0 -> x4, waiting for transfers between devices: none -> 29.6 us  [gather(): return lax.all_gather(mat, 'tp', axis=0, tiled=True)]
  transfers between devices with their start and end apart: 4 -> 30, of which waited for: 4 -> 16; matrix products, arithmetic and copies ran while one was open for 9% -> 18% of each run, Pallas kernels for 0% -> 16%
where the time goes in v1:
time: 704 us; the launch traced here: 694 us
  waiting for transfers between devices  305 us (43%)
  matrix products  163 us (23%)
  Pallas kernels  112 us (16%)
  local copies, waits for them, and re-layouts  37.9 us (5%)
  other arithmetic  32.9 us (5%)
  starting transfers between devices  28.8 us (4%)
  between operations  15.1 us (2%)
    dot_general x12, matrix products, dot32(): return lax.dot_general(lhs, rhs, dims, preferred_element_type=jnp.float32)  163 us
    ppermute x2, waiting for transfers between devices, exchange(): far = lax.ppermute(rows, 'tp', far_pairs)  156 us
    reduce_scatter x4, waiting for transfers between devices, scatter(): return lax.psum_scatter(mat, 'tp', scatter_dimension=0, tiled=True)  49.5 us
    pallas_call x1, Pallas kernels, attention_backward(): pl.pallas_call(functools.partial(attn_bwd_kernel, head_dim, head_dim ** (...  38.7 us
    pallas_call x1, Pallas kernels, attention_forward(): pl.pallas_call(functools.partial(attn_fwd_kernel, head_dim, head_dim ** (...  36.9 us
    pallas_call x4, Pallas kernels, place_pair(): pl.pallas_call(place_kernel, grid_spec=pltpu.PrefetchScalarGridSpec(num_s...  36.1 us
    all_gather x4, waiting for transfers between devices, gather(): return lax.all_gather(mat, 'tp', axis=0, tiled=True)  29.6 us
    ppermute x2, waiting for transfers between devices, ring_sum(): low = lax.ppermute(opposite[:half], axis, upward)  19.5 us
  transfers between devices with their start and end apart: 30, of which 16 were waited for; matrix products, arithmetic and copies ran while one was open for 18% of the time, Pallas kernels for 16%

profile of v1, /device:TPU:0, one launch (start us, length us, event | category | flops | bytes accessed | tf_op | source)
XLA Modules:
  0.0 694.0 jit_solution(497688165769758087)
XLA Ops:
  27.6 15.5 %all-gather.5.cloned.1.call-done = bf16[2304,768]{1,0:T(8,128)(2,1)} async-done(((bf16[576,768]{1,0:T(8,128)(2,1)}), bf16[2304,768]{1,0:T(8,128)(2,1)}) %all-gather.5.cloned.1.call-update) | async-done | bytes 3538960 | tf_op jit(solution)/shard_map/all_gather | solution.py:263
  43.1 11.9 %fusion.10.qkv_ref = bf16[2304,2048]{1,0:T(8,128)(2,1)} fusion(bf16[2048,768]{1,0:T(8,128)(2,1)S(1)} %fusion.41, bf16[2304,768]{1,0:T(8,128)(2,1)} %all-gather.5.cloned.1.call-done), kind=kOutput, calls=%fused_computation.16 | convolution fusion | flops 7252475904 | bytes 16121856 | tf_op jit(solution)/shard_map/dot_general | solution.py:24
  55.0 36.9 %attn_fwd.1 = (bf16[768,2048]{1,0:T(8,128)(2,1)}, f32[4,6,2,512]{3,2,1,0:T(2,128)}) custom-call(s32[4,1,512]{2,1,0:T(1,128)} %broadcast_in_dim.10.seg_q_ref, s32[4,512,1]{2,1,0:T(8,128)} %copy.26.seg_k_ref, bf16[2304,2048]{1,0:T(8,128)(2,1)} %fusion.10.qkv_ref), custom_call_target="tpu_custom_call" | custom-call | flops 12884901888 | bytes 12582912 | tf_op jit(solution)/shard_map/attn_fwd/pallas_call | solution.py:128
  101.4 24.4 %multiply_convert_fusion = (bf16[2048,3072]{1,0:T(8,128)(2,1)}, f32[2048,3072]{1,0:T(8,128)}) fusion(bf16[2048,768]{1,0:T(8,128)(2,1)} %fusion.21, bf16[3072,768]{0,1:T(8,128)(2,1)} %all-gather.9.cloned.1.call-done), kind=kOutput, calls=%fused_computation.14 | convolution fusion | flops 9720299520 | bytes 45613056 | tf_op jit(solution)/shard_map/dot_general | solution.py:24
  125.9 14.2 %all-gather.11.cloned.1.call-done = bf16[3072,768]{1,0:T(8,128)(2,1)} async-done(((bf16[768,768]{1,0:T(8,128)(2,1)}), bf16[3072,768]{1,0:T(8,128)(2,1)}) %all-gather.11.cloned.1.call-update) | async-done | bytes 4718608 | tf_op jit(solution)/shard_map/all_gather | solution.py:263
  140.0 15.5 %fusion.35.one_ref = bf16[2048,768]{1,0:T(8,128)(2,1)} fusion(bf16[2048,768]{1,0:T(8,128)(2,1)S(1)} %get-tuple-element.85, bf16[2048,3072]{1,0:T(8,128)(2,1)} %get-tuple-element.27, bf16[3072,768]{1,0:T(8,128)(2,1)} %all-gather.11.cloned.1.call-done), kind=kOutput, calls=%fused_computation.48 | convolution fusion | flops 9671540736 | bytes 23592960 | tf_op jit(solution)/shard_map/dot_general | solution.py:24
  155.6 12.2 %convolution_convert_fusion.2 = bf16[3072,768]{1,0:T(8,128)(2,1)} fusion(bf16[2048,3072]{1,0:T(8,128)(2,1)S(1)} %copy-done.24, bf16[2048,768]{1,0:T(8,128)(2,1)S(1)} %bitcast.122), kind=kOutput, calls=%fused_computation.61 | convolution fusion | flops 9666035712 | bytes 20447232 | tf_op jit(solution)/shard_map/dot_general | solution.py:24
  167.8 31.2 %fusion.2 = bf16[2048,3072]{1,0:T(8,128)(2,1)} fusion(f32[2048,3072]{1,0:T(8,128)} %get-tuple-element.87, bf16[2048,768]{1,0:T(8,128)(2,1)} %bitcast.121, bf16[3072,768]{1,0:T(8,128)(2,1)} %all-gather.11.cloned.1.call-done), kind=kOutput, calls=%fused_computation.6 | convolution fusion | flops 9802088448 | bytes 45613056 | tf_op jit(solution)/shard_map/dot_general | solution.py:24
  199.0 14.7 %convolution_convert_fusion.1 = bf16[3072,768]{1,0:T(8,128)(2,1)} fusion(bf16[2048,3072]{1,0:T(8,128)(2,1)} %fusion.2, bf16[2048,768]{1,0:T(8,128)(2,1)S(1)} %copy-done.12), kind=kOutput, calls=%fused_computation.60 | convolution fusion | flops 9666035712 | bytes 20447232 | tf_op jit(solution)/shard_map/dot_general | solution.py:24
  213.7 15.4 %fusion.28 = (bf16[768]{0:T(1024)(128)(2,1)S(1)}, f32[2048]{0:T(1024)S(1)}, f32[2048]{0:T(1024)S(1)}, bf16[2048,768]{1,0:T(8,128)(2,1)S(1)}) fusion(bf16[2048,768]{1,0:T(8,128)(2,1)S(1)} %get-tuple-element.85, f32[2048]{0:T(1024)S(1)} %add_rsqrt_fusion, f32[2048]{0:T(1024)S(1)} %broadcast_multiply_fusion.4, f32[768]{0:T(1024)S(1)} %convert_element_type.197, ...), kind=kOutput, calls=%fused_computation.41 | convolution fusion | flops 9680972800 | bytes 23630336 | tf_op jit(solution)/shard_map/dot_general | solution.py:24
  244.8 38.7 %attn_bwd.1 = bf16[2304,2048]{1,0:T(8,128)(2,1)} custom-call(s32[4,1,512]{2,1,0:T(1,128)} %broadcast_in_dim.10.seg_q_ref, s32[4,512,1]{2,1,0:T(8,128)} %copy.26.seg_k_ref, bf16[2304,2048]{1,0:T(8,128)(2,1)} %fusion.10.qkv_ref, bf16[768,2048]{1,0:T(8,128)(2,1)} %get-tuple-element.25.out_ref, f32[4,6,2,512]{3,2,1,0:T(2,128)} %get-tuple-element.32.lse_ref, ...), custom_call_target="tpu_custom_call" | custom-call | flops 32212254720 | bytes 25165824 | tf_op jit(solution)/shard_map/attn_bwd/pallas_call | solution.py:145
  283.5 14.0 %fusion.34 = (bf16[768]{0:T(1024)(128)(2,1)S(1)}, f32[2048]{0:T(1024)S(1)}, f32[2048]{0:T(1024)S(1)}, bf16[2048,768]{1,0:T(8,128)(2,1)S(1)}) fusion(f32[2048]{0:T(1024)S(1)} %bitcast.138, f32[2048]{0:T(1024)S(1)} %bitcast.141, bf16[16,512,768]{2,1,0:T(8,128)(2,1)} %param.9, s32[]{:T(128)S(6)} %select_n.53, f32[768]{0:T(1024)S(1)} %copy-done.19, ...), kind=kOutput, calls=%fused_computation.47 | convolution fusion | flops 7265053696 | bytes 19304964 | tf_op jit(solution)/shard_map/dot_general | solution.py:24
  304.3 8.0 %convolution_convert_fusion.3 = bf16[2304,768]{1,0:T(8,128)(2,1)S(1)} fusion(bf16[2304,2048]{1,0:T(8,128)(2,1)S(1)} %copy-done.23, bf16[2048,768]{1,0:T(8,128)(2,1)S(1)} %copy-done.11), kind=kOutput, calls=%fused_computation.62 | convolution fusion | flops 7249526784 | bytes 16121856 | tf_op jit(solution)/shard_map/dot_general | solution.py:24
  314.6 49.5 %reduce-scatter.5.cloned.1.call-done = bf16[768,768]{1,0:T(8,128)(2,1)} async-done(((bf16[3072,768]{1,0:T(8,128)(2,1)}), bf16[768,768]{1,0:T(8,128)(2,1)}) %reduce-scatter.5.cloned.1.call-update) | async-done | bytes 1179664 | tf_op jit(solution)/shard_map/reduce_scatter | solution.py:266
  366.7 89.6 %collective-permute-done.3.one_ref = bf16[2048,768]{1,0:T(8,128)(2,1)} collective-permute-done((bf16[2048,768]{1,0:T(8,128)(2,1)S(1)}, bf16[2048,768]{1,0:T(8,128)(2,1)}, u32[]{:S(2)}, u32[]{:S(2)}) %collective-permute-start.3) | collective-permute-done | bytes 3145760 | tf_op jit(solution)/shard_map/ppermute | solution.py:269
  456.3 66.1 %collective-permute-done.one_ref = bf16[2048,768]{1,0:T(8,128)(2,1)} collective-permute-done((bf16[2048,768]{1,0:T(8,128)(2,1)}, bf16[2048,768]{1,0:T(8,128)(2,1)}, u32[]{:S(2)}, u32[]{:S(2)}) %collective-permute-start) | collective-permute-done | bytes 3145760 | tf_op jit(solution)/shard_map/ppermute | solution.py:269
  529.2 9.4 %collective-permute-done.14 = bf16[208,768]{1,0:T(8,128)(2,1)} collective-permute-done((bf16[208,768]{1,0:T(8,128)(2,1)}, bf16[208,768]{1,0:T(8,128)(2,1)}, u32[]{:S(2)}, u32[]{:S(2)}) %collective-permute-start.14) | collective-permute-done | bytes 319520 | tf_op jit(solution)/shard_map/ppermute | solution.py:216
  550.2 15.5 %collective-permute-done.15 = bf16[432,768]{1,0:T(8,128)(2,1)S(1)} collective-permute-done((bf16[432,768]{1,0:T(8,128)(2,1)S(1)}, bf16[432,768]{1,0:T(8,128)(2,1)S(1)}, u32[]{:S(2)}, u32[]{:S(2)}) %collective-permute-start.15) | collective-permute-done | bytes 663584 | tf_op jit(solution)/shard_map/ppermute | solution.py:220
  568.0 13.5 %collective-permute-done.17 = bf16[432,768]{1,0:T(8,128)(2,1)} collective-permute-done((bf16[432,768]{1,0:T(8,128)(2,1)}, bf16[432,768]{1,0:T(8,128)(2,1)}, u32[]{:S(2)}, u32[]{:S(2)}) %collective-permute-start.17) | collective-permute-done | bytes 663584 | tf_op jit(solution)/shard_map/ppermute | solution.py:221
  589.9 9.0 %place_pair.6.rest_0_ = bf16[4,2048,768]{2,1,0:T(8,128)(2,1)} custom-call(s32[2]{0:T(128)} %get-tuple-element.91.slots_ref, bf16[2048,768]{1,0:T(8,128)(2,1)} %fusion.32.one_ref, bf16[2048,768]{1,0:T(8,128)(2,1)} %collective-permute-done.5.two_ref), custom_call_target="tpu_custom_call" | custom-call | bytes 12582912 | tf_op jit(solution)/shard_map/place_pair/pallas_call | solution.py:184
  598.8 9.0 %place_pair.4.rest_0_ = bf16[4,2048,768]{2,1,0:T(8,128)(2,1)} custom-call(s32[2]{0:T(128)} %get-tuple-element.91.slots_ref, bf16[2048,768]{1,0:T(8,128)(2,1)} %fusion.35.one_ref, bf16[2048,768]{1,0:T(8,128)(2,1)} %collective-permute-done.2.two_ref), custom_call_target="tpu_custom_call" | custom-call | bytes 12582912 | tf_op jit(solution)/shard_map/place_pair/pallas_call | solution.py:184
  607.8 9.0 %place_pair.7 = bf16[4,2048,768]{2,1,0:T(8,128)(2,1)} custom-call(s32[2]{0:T(128)} %get-tuple-element.90.slots_ref, bf16[2048,768]{1,0:T(8,128)(2,1)} %collective-permute-done.3.one_ref, bf16[2048,768]{1,0:T(8,128)(2,1)} %collective-permute-done.4.two_ref, bf16[4,2048,768]{2,1,0:T(8,128)(2,1)} %place_pair.6.rest_0_), custom_call_target="tpu_custom_call", output_to_operand_aliasing={{}: (3, {})} | custom-call | bytes 12582912 | tf_op jit(solution)/shard_map/place_pair/pallas_call | solution.py:184
  616.8 9.1 %place_pair.5 = bf16[4,2048,768]{2,1,0:T(8,128)(2,1)} custom-call(s32[2]{0:T(128)} %get-tuple-element.90.slots_ref, bf16[2048,768]{1,0:T(8,128)(2,1)} %collective-permute-done.one_ref, bf16[2048,768]{1,0:T(8,128)(2,1)} %collective-permute-done.1.two_ref, bf16[4,2048,768]{2,1,0:T(8,128)(2,1)} %place_pair.4.rest_0_), custom_call_target="tpu_custom_call", output_to_operand_aliasing={{}: (3, {})} | custom-call | bytes 12582912 | tf_op jit(solution)/shard_map/place_pair/pallas_call | solution.py:184
  637.3 10.1 %collective-permute-done.6 = bf16[80,768]{1,0:T(8,128)(2,1)S(1)} collective-permute-done((bf16[80,768]{1,0:T(8,128)(2,1)S(1)}, bf16[80,768]{1,0:T(8,128)(2,1)S(1)}, u32[]{:S(2)}, u32[]{:S(2)}) %collective-permute-start.6) | collective-permute-done | bytes 122912 | tf_op jit(solution)/shard_map/ppermute | solution.py:216
  (174 shorter events, 136.7 us)
Async XLA Ops:
  7.2 35.9 %all-gather.5.cloned.1.call-start = ((), (), s32[]{:S(2)}) async-start(), calls=%async_computation.4 | async-start | bytes 4423680 | tf_op jit(solution)/shard_map/all_gather | solution.py:263
  7.9 84.0 %all-gather.7.cloned.1.call-start = ((), (), s32[]{:S(2)}) async-start(), calls=%async_computation.5 | async-start | bytes 1474560 | tf_op jit(solution)/shard_map/all_gather | solution.py:263
  8.7 92.8 %all-gather.9.cloned.1.call-start = ((), (), s32[]{:S(2)}) async-start(), calls=%async_computation.6 | async-start | bytes 5898240 | tf_op jit(solution)/shard_map/all_gather | solution.py:263
  9.4 130.6 %all-gather.11.cloned.1.call-start = ((), (), s32[]{:S(2)}) async-start(), calls=%async_computation.7 | async-start | bytes 5898240 | tf_op jit(solution)/shard_map/all_gather | solution.py:263
  10.0 304.6 %reduce-scatter.9.cloned.1.call-start = ((), (), s32[]{:S(2)}) async-start(), calls=%async_computation.10 | async-start | bytes 1474560 | tf_op jit(solution)/shard_map/reduce_scatter | solution.py:266
  237.4 77.2 %reduce-scatter.7.cloned.1.call-start = ((), (), s32[]{:S(2)}) async-start(), calls=%async_computation.9 | async-start | bytes 5898240 | tf_op jit(solution)/shard_map/reduce_scatter | solution.py:266
  237.9 126.1 %reduce-scatter.5.cloned.1.call-start = ((), (), s32[]{:S(2)}) async-start(), calls=%async_computation.8 | async-start | bytes 5898240 | tf_op jit(solution)/shard_map/reduce_scatter | solution.py:266
  238.7 393.5 %reduce-scatter.11.cloned.1.call-start = ((), (), s32[]{:S(2)}) async-start(), calls=%async_computation.11 | async-start | bytes 4915200 | tf_op jit(solution)/shard_map/reduce_scatter | solution.py:266
  364.1 92.2 %collective-permute-start.3 = (bf16[2048,768]{1,0:T(8,128)(2,1)S(1)}, bf16[2048,768]{1,0:T(8,128)(2,1)}, u32[]{:S(2)}, u32[]{:S(2)}) collective-permute-start(bf16[2048,768]{1,0:T(8,128)(2,1)S(1)} %copy-done.6), channel_id=1, source_target_pairs={{0,2},{1,3},{2,0},{3,1},{4,6},{5,7},{6,4},{7,5},{8,10},{9,11},{10,... | collective-permute-start | bytes 9437192 | tf_op jit(solution)/shard_map/ppermute | solution.py:269
  364.5 157.9 %collective-permute-start = (bf16[2048,768]{1,0:T(8,128)(2,1)}, bf16[2048,768]{1,0:T(8,128)(2,1)}, u32[]{:S(2)}, u32[]{:S(2)}) collective-permute-start(bf16[2048,768]{1,0:T(8,128)(2,1)} %fusion.35.one_ref), channel_id=1, source_target_pairs={{0,2},{1,3},{2,0},{3,1},{4,6},{5,7},{6,4},{7,5},{8,10},{9,11},{10,... | collective-permute-start | bytes 9437192 | tf_op jit(solution)/shard_map/ppermute | solution.py:269
  366.2 218.1 %collective-permute-start.5 = (bf16[2048,768]{1,0:T(8,128)(2,1)S(1)}, bf16[2048,768]{1,0:T(8,128)(2,1)}, u32[]{:S(2)}, u32[]{:S(2)}) collective-permute-start(bf16[2048,768]{1,0:T(8,128)(2,1)S(1)} %copy-done.6), channel_id=1, source_target_pairs={{0,1},{1,0},{2,3},{3,2},{4,5},{5,4},{6,7},{7,6},{8,9},{9,8},{10,11... | collective-permute-start | bytes 9437192 | tf_op jit(solution)/shard_map/ppermute | solution.py:270
  366.2 232.7 %collective-permute-start.2 = (bf16[2048,768]{1,0:T(8,128)(2,1)}, bf16[2048,768]{1,0:T(8,128)(2,1)}, u32[]{:S(2)}, u32[]{:S(2)}) collective-permute-start(bf16[2048,768]{1,0:T(8,128)(2,1)} %fusion.35.one_ref), channel_id=1, source_target_pairs={{0,1},{1,0},{2,3},{3,2},{4,5},{5,4},{6,7},{7,6},{8,9},{9,8},{10,11... | collective-permute-start | bytes 9437192 | tf_op jit(solution)/shard_map/ppermute | solution.py:270
  456.3 151.5 %collective-permute-start.4 = (bf16[2048,768]{1,0:T(8,128)(2,1)}, bf16[2048,768]{1,0:T(8,128)(2,1)}, u32[]{:S(2)}, u32[]{:S(2)}) collective-permute-start(bf16[2048,768]{1,0:T(8,128)(2,1)} %collective-permute-done.3.one_ref), channel_id=1, source_target_pairs={{0,1},{1,0},{2,3},{3,2},{4,5},{5,4},{6,7},{7,6},{8,9},{9,8},{10,11... | collective-permute-start | bytes 9437192 | tf_op jit(solution)/shard_map/ppermute | solution.py:271
  522.4 94.4 %collective-permute-start.1 = (bf16[2048,768]{1,0:T(8,128)(2,1)}, bf16[2048,768]{1,0:T(8,128)(2,1)}, u32[]{:S(2)}, u32[]{:S(2)}) collective-permute-start(bf16[2048,768]{1,0:T(8,128)(2,1)} %collective-permute-done.one_ref), channel_id=1, source_target_pairs={{0,1},{1,0},{2,3},{3,2},{4,5},{5,4},{6,7},{7,6},{8,9},{9,8},{10,11... | collective-permute-start | bytes 9437192 | tf_op jit(solution)/shard_map/ppermute | solution.py:271
  526.6 12.1 %collective-permute-start.14 = (bf16[208,768]{1,0:T(8,128)(2,1)}, bf16[208,768]{1,0:T(8,128)(2,1)}, u32[]{:S(2)}, u32[]{:S(2)}) collective-permute-start(bf16[208,768]{1,0:T(8,128)(2,1)} %get-tuple-element.72), channel_id=1, source_target_pairs={{0,4},{4,8},{8,12},{12,0},{1,5},{5,9},{9,13},{13,1},{2,6},{6,10},{... | collective-permute-start | bytes 958472 | tf_op jit(solution)/shard_map/ppermute | solution.py:216
  548.2 17.4 %collective-permute-start.15 = (bf16[432,768]{1,0:T(8,128)(2,1)S(1)}, bf16[432,768]{1,0:T(8,128)(2,1)S(1)}, u32[]{:S(2)}, u32[]{:S(2)}) collective-permute-start(bf16[432,768]{1,0:T(8,128)(2,1)S(1)} %pad_maximum_fusion.2), channel_id=1, source_target_pairs={{0,4},{4,8},{8,12},{12,0},{1,5},{5,9},{9,13},{13,1},{2,6},{6,10},{... | collective-permute-start | bytes 1990664 | tf_op jit(solution)/shard_map/ppermute | solution.py:220
  566.5 15.0 %collective-permute-start.17 = (bf16[432,768]{1,0:T(8,128)(2,1)}, bf16[432,768]{1,0:T(8,128)(2,1)}, u32[]{:S(2)}, u32[]{:S(2)}) collective-permute-start(bf16[432,768]{1,0:T(8,128)(2,1)} %pad_maximum_fusion.3), channel_id=1, source_target_pairs={{0,12},{4,0},{8,4},{12,8},{1,13},{5,1},{9,5},{13,9},{2,14},{6,2},{... | collective-permute-start | bytes 1990664 | tf_op jit(solution)/shard_map/ppermute | solution.py:221
  584.3 41.6 %collective-permute-start.19 = (bf16[432,768]{1,0:T(8,128)(2,1)}, bf16[432,768]{1,0:T(8,128)(2,1)}, u32[]{:S(2)}, u32[]{:S(2)}) collective-permute-start(bf16[432,768]{1,0:T(8,128)(2,1)} %get-tuple-element.67), channel_id=1, source_target_pairs={{0,4},{4,8},{8,12},{12,0},{1,5},{5,9},{9,13},{13,1},{2,6},{6,10},{... | collective-permute-start | bytes 1990664 | tf_op jit(solution)/shard_map/ppermute | solution.py:223
  585.9 41.7 %collective-permute-start.18 = (bf16[432,768]{1,0:T(8,128)(2,1)}, bf16[432,768]{1,0:T(8,128)(2,1)S(1)}, u32[]{:S(2)}, u32[]{:S(2)}) collective-permute-start(bf16[432,768]{1,0:T(8,128)(2,1)} %get-tuple-element.67), channel_id=1, source_target_pairs={{0,12},{4,0},{8,4},{12,8},{1,13},{5,1},{9,5},{13,9},{2,14},{6,2},{... | collective-permute-start | bytes 1990664 | tf_op jit(solution)/shard_map/ppermute | solution.py:224
  627.6 26.0 %collective-permute-start.20 = (bf16[208,768]{1,0:T(8,128)(2,1)}, bf16[208,768]{1,0:T(8,128)(2,1)}, u32[]{:S(2)}, u32[]{:S(2)}) collective-permute-start(bf16[208,768]{1,0:T(8,128)(2,1)} %slice.129), channel_id=1, source_target_pairs={{0,4},{4,8},{8,12},{12,0},{1,5},{5,9},{9,13},{13,1},{2,6},{6,10},{... | collective-permute-start | bytes 958472 | tf_op jit(solution)/shard_map/ppermute | solution.py:225
  628.4 26.2 %collective-permute-start.21 = (bf16[224,768]{1,0:T(8,128)(2,1)}, bf16[224,768]{1,0:T(8,128)(2,1)}, u32[]{:S(2)}, u32[]{:S(2)}) collective-permute-start(bf16[224,768]{1,0:T(8,128)(2,1)} %slice.130), channel_id=1, source_target_pairs={{0,12},{4,0},{8,4},{12,8},{1,13},{5,1},{9,5},{13,9},{2,14},{6,2},{... | collective-permute-start | bytes 1032200 | tf_op jit(solution)/shard_map/ppermute | solution.py:226
  633.3 14.0 %collective-permute-start.6 = (bf16[80,768]{1,0:T(8,128)(2,1)S(1)}, bf16[80,768]{1,0:T(8,128)(2,1)S(1)}, u32[]{:S(2)}, u32[]{:S(2)}) collective-permute-start(bf16[80,768]{1,0:T(8,128)(2,1)S(1)} %get-tuple-element.78), channel_id=1, source_target_pairs={{0,4},{4,8},{8,12},{12,0},{1,5},{5,9},{9,13},{13,1},{2,6},{6,10},{... | collective-permute-start | bytes 368648 | tf_op jit(solution)/shard_map/ppermute | solution.py:216
  633.4 14.0 %collective-permute-start.8 = (bf16[80,768]{1,0:T(8,128)(2,1)S(1)}, bf16[80,768]{1,0:T(8,128)(2,1)S(1)}, u32[]{:S(2)}, u32[]{:S(2)}) collective-permute-start(bf16[80,768]{1,0:T(8,128)(2,1)S(1)} %get-tuple-element.80), channel_id=1, source_target_pairs={{0,12},{4,0},{8,4},{12,8},{1,13},{5,1},{9,5},{13,9},{2,14},{6,2},{... | collective-permute-start | bytes 368648 | tf_op jit(solution)/shard_map/ppermute | solution.py:217
  662.2 14.2 %collective-permute-start.10 = (bf16[160,768]{1,0:T(8,128)(2,1)S(1)}, bf16[160,768]{1,0:T(8,128)(2,1)S(1)}, u32[]{:S(2)}, u32[]{:S(2)}) collective-permute-start(bf16[160,768]{1,0:T(8,128)(2,1)S(1)} %get-tuple-element.69), channel_id=1, source_target_pairs={{0,12},{4,0},{8,4},{12,8},{1,13},{5,1},{9,5},{13,9},{2,14},{6,2},{... | collective-permute-start | bytes 737288 | tf_op jit(solution)/shard_map/ppermute | solution.py:224
  (31 other events, 450.3 us)
Sparse Core Ops, SparseCore 0:
  9.6 33.4 all-gather.4
  44.6 17.4 all-gather.6
  63.7 37.4 all-gather.8
  102.5 37.4 all-gather.10
  237.5 25.6 reduce-scatter.8
  265.5 47.9 reduce-scatter.6
  316.0 47.9 reduce-scatter.4
  366.6 65.1 reduce-scatter.10
